TPU v7x, 32 devices: a whole 2x2x4 slice. The times are simulated.
32 devices in a mesh: row: 8 (over z, x), col: 4 (over y, core).
Axes of the slice: x: 2, y: 2, z: 4, core: 2. Of those that a mesh axis runs over, the one named last changes fastest.
Arguments:
- momentum: float32 [5120, 13312], P('row', 'col')
- gradient: float32 [5120, 13312], P('row', 'col'), may hold values from -6 to 6
Outputs:
- new_momentum: float32 [5120, 13312], P('row', 'col')
- update: float32 [5120, 13312], P('row', 'col')
All inputs are finite; a program needn't handle non-finite values.
Results may differ from a plain program's by a relative error of at most 0.00073.
The roundings to bfloat16 on the way count: a program that leaves them out, or rounds other values in their place, can miss the bound.
Values may be sent and summed in bfloat16 or wider, within the bound.
No kernel may reach another device: no remote copies, remote signals or barrier semaphores. Data moves between devices by JAX's collectives and lax.ppermute only.
A program may use at most 128 MiB of HBM per device.

v0:
```python
import jax
import jax.numpy as jnp
from jax import lax
from jax.sharding import PartitionSpec as P

D = 5120
FF_WIN = 13312


def gram_rows(left, right):
    return lax.dot_general(
        left, right, (((1,), (1,)), ((), ())), preferred_element_type=jnp.float32
    )


def shards(momentum, gradient):
    new_momentum = 0.95 * momentum + gradient
    squares = lax.psum(jnp.sum(new_momentum * new_momentum), ("row", "col"))
    normed = new_momentum / (jnp.sqrt(3.0 * squares / D) + 1e-07)
    rounded = normed.astype(jnp.bfloat16)
    gathered = lax.all_gather(rounded, "row", axis=0, tiled=True)
    partial_value = gram_rows(rounded, gathered)
    share = lax.psum_scatter(partial_value, "col", scatter_dimension=1, tiled=True)
    gram_rounded = lax.all_gather(share.astype(jnp.bfloat16), "col", axis=1, tiled=True)
    product = jnp.dot(gram_rounded, gathered, preferred_element_type=jnp.float32)
    update = (1.5 * normed - 0.5 * product) * jnp.sqrt(jnp.float32(3 * FF_WIN))
    return (new_momentum, update)


def solution(mesh):
    placed = (P("row", "col"), P("row", "col"))
    return jax.shard_map(
        shards,
        mesh=mesh,
        in_specs=placed,
        out_specs=(P("row", "col"), P("row", "col")),
        check_vma=False,
    )
```

profile of v0, /device:TPU:0, one launch (start us, length us, event | category | flops | bytes accessed | tf_op | source)
XLA Modules:
  0.0 936.4 jit_solution(967690952968783723)
XLA Ops:
  7.2 0.0 all-gather.3.cloned.1.call-start
  7.2 12.0 %multiply_reduce_fusion = (f32[]{:T(128)}, f32[640,3328]{1,0:T(8,128)}) fusion(f32[640,3328]{1,0:T(8,128)} %param.3, f32[640,3328]{1,0:T(8,128)} %param.2), kind=kLoop, calls=%fused_computation.1 | loop fusion | flops 8519679 | bytes 25559044 | tf_op jit(solution)/shard_map/reduce_sum | solution.py:18
  19.2 42.2 %psum.7 = f32[]{:T(128)} all-reduce(f32[]{:T(128)} %get-tuple-element.2), channel_id=1, replica_groups=mesh['row'=8,'col'=4] {'row','col'}, use_global_device_ids=true, to_apply=%region_1.0 | all-reduce | flops 1 | bytes 8 | tf_op jit(solution)/shard_map/psum | solution.py:18
  62.1 6.1 fusion
  68.1 0.0 all-gather.3.cloned.1.call-update
  68.2 0.0 reduce-scatter.2.cloned.1.call-start
  68.2 647.6 %all-gather.3.cloned.1.call-done = bf16[5120,3328]{1,0:T(8,128)(2,1)} async-done(((bf16[640,3328]{1,0:T(8,128)(2,1)}), bf16[5120,3328]{1,0:T(8,128)(2,1)}) %all-gather.3.cloned.1.call-update) | async-done | bytes 34078736 | tf_op jit(solution)/shard_map/all_gather | solution.py:21
  715.8 29.1 %fusion.1 = f32[640,5120]{1,0:T(8,128)} fusion(bf16[640,3328]{1,0:T(8,128)(2,1)} %fusion, bf16[5120,3328]{1,0:T(8,128)(2,1)} %all-gather.3.cloned.1.call-done), kind=kOutput, calls=%fused_computation.5 | convolution fusion | flops 21810380800 | bytes 51445760 | tf_op jit(solution)/shard_map/dot_general | solution.py:11
  744.9 0.0 reduce-scatter.2.cloned.1.call-update
  744.9 0.0 all-gather.5.cloned.1.call-start
  745.0 100.5 %reduce-scatter.2.cloned.1.call-done = f32[640,1280]{1,0:T(8,128)} async-done(((f32[640,5120]{1,0:T(8,128)}), f32[640,1280]{1,0:T(8,128)}) %reduce-scatter.2.cloned.1.call-update) | async-done | bytes 3276816 | tf_op jit(solution)/shard_map/reduce_scatter | solution.py:23
  845.5 3.2 convert_element_type.7
  848.7 0.0 all-gather.5.cloned.1.call-update
  848.8 48.0 %all-gather.5.cloned.1.call-done = bf16[640,5120]{1,0:T(8,128)(2,1)} async-done(((bf16[640,1280]{1,0:T(8,128)(2,1)}), bf16[640,5120]{1,0:T(8,128)(2,1)}) %all-gather.5.cloned.1.call-update) | async-done | bytes 6553616 | tf_op jit(solution)/shard_map/all_gather | solution.py:24
  896.8 33.1 %subtract_multiply_fusion = f32[640,3328]{1,0:T(8,128)} fusion(bf16[640,5120]{1,0:T(8,128)(2,1)} %all-gather.5.cloned.1.call-done, bf16[5120,3328]{1,0:T(8,128)(2,1)} %all-gather.3.cloned.1.call-done, f32[640,3328]{1,0:T(8,128)} %get-tuple-element.3, f32[]{:T(128)S(6)} %add.11), kind=kOutput, calls=%fused_computation | convolution fusion | flops 21821030400 | bytes 57671684 | tf_op jit(solution)/shard_map/dot_general | solution.py:25
Async XLA Ops:
  7.2 708.6 %all-gather.3.cloned.1.call-start = ((), (), s32[]{:S(2)}) async-start(), calls=%async_computation.1 | async-start | bytes 38338560 | tf_op jit(solution)/shard_map/all_gather | solution.py:21
  68.2 777.3 %reduce-scatter.2.cloned.1.call-start = ((), (), s32[]{:S(2)}) async-start(), calls=%async_computation.2 | async-start | bytes 16384000 | tf_op jit(solution)/shard_map/reduce_scatter | solution.py:23
  744.9 151.8 %all-gather.5.cloned.1.call-start = ((), (), s32[]{:S(2)}) async-start(), calls=%async_computation.3 | async-start | bytes 8192000 | tf_op jit(solution)/shard_map/all_gather | solution.py:24
Sparse Core Ops, SparseCore 0:
  68.3 647.4 all-gather.2
  745.1 100.3 reduce-scatter.1
  848.9 47.8 all-gather.4
where the time goes:
time: 937 us; the launch traced here: 936 us
  waiting for transfers between devices  796 us (85%)
  matrix products  62.3 us (7%)
  blocking collectives  42.2 us (5%)
  other arithmetic  21.3 us (2%)
  between operations  14.4 us (2%)
    all_gather x1, waiting for transfers between devices, shards(): gathered = lax.all_gather(rounded, 'row', axis=0, tiled=True)  648 us
    reduce_scatter x1, waiting for transfers between devices, shards(): lax.psum_scatter(partial_value, 'col', scatter_dimension=1, tiled=True)  101 us
    all_gather x1, waiting for transfers between devices, shards(): lax.all_gather(share.astype(jnp.bfloat16), 'col', axis=1, tiled=True)  48 us
    psum x1, blocking collectives, shards(): squares = lax.psum(jnp.sum(new_momentum * new_momentum), ('row', 'col'))  42.2 us
    dot_general x1, matrix products, shards(): jnp.dot(gram_rounded, gathered, preferred_element_type=jnp.float32)  33.1 us
    dot_general x1, matrix products, gram_rows(): lax.dot_general(left, right, (((1,), (1,)), ((), ())), preferred_element_...  29.1 us
  transfers between devices with their start and end apart: 3, of which 3 were waited for; matrix products, arithmetic and copies ran while one was open for 0% of the time, Pallas kernels for 0%

commit v1 on v0

v1 whole, which is shorter than its diff:
```python
import jax
import jax.numpy as jnp
from jax import lax
from jax.experimental import pallas as pl
from jax.experimental.pallas import tpu as pltpu
from jax.sharding import PartitionSpec as P


D = 5120
FF_WIN = 13312


def cycle(mesh):
    places = [tuple(d.coords) for d in mesh.devices[:, 0]]
    n = len(places)
    first = [a != b for a, b in zip(places[0], places[1 % n])]
    minor = n
    for i, place in enumerate(places):
        if any(a != b and not f for a, b, f in zip(place, places[0], first)):
            minor = i
            break
    major = n // minor
    order = []
    for i in range(major):
        along = range(1, minor) if i % 2 == 0 else range(minor - 1, 0, -1)
        order += [i * minor + j for j in along]
    order += [i * minor for i in range(major - 1, -1, -1)]
    return order


def flip(x, bit, n, axis):
    return lax.ppermute(x, axis, [(i, i ^ bit) for i in range(n)])


def bits_of(n):
    return [1 << k for k in range(n.bit_length() - 1)]


def total(x, axis, n):
    for bit in bits_of(n):
        x = x + flip(x, bit, n, axis)
    return x


def dot_rows(left, right):
    return lax.dot_general(left, right, (((1,), (1,)), ((), ())), preferred_element_type=jnp.float32)


def held(x):
    return pl.BlockSpec(x.shape, lambda *_: (0,) * x.ndim, pipeline_mode=pl.Buffered(1))


def grams(pairs):
    given = []
    for pair in pairs:
        for block in pair:
            if not any(block is g for g in given):
                given.append(block)
    at = lambda block: next(i for i, g in enumerate(given) if g is block)
    flat = [x for block in given for x in block]
    rows = flat[0].shape[0]

    def kernel(*refs):
        out = refs[-1]
        for p, (left, right) in enumerate(pairs):
            i, j = 2 * at(left), 2 * at(right)

            @pl.when(pl.program_id(0) == p)
            def _():
                out[0] = dot_rows(refs[i][...], refs[j][...]) + dot_rows(refs[i + 1][...], refs[j + 1][...])

    width = sum(x.shape[1] for x in given[0])
    return pl.pallas_call(
        kernel,
        grid=(len(pairs),),
        in_specs=[held(x) for x in flat],
        out_specs=pl.BlockSpec((1, rows, rows), lambda p: (p, 0, 0)),
        out_shape=jax.ShapeDtypeStruct((len(pairs), rows, rows), jnp.float32),
        cost_estimate=pl.CostEstimate(
            flops=2 * len(pairs) * rows * rows * width,
            bytes_accessed=2 * len(flat) * flat[0].size + 4 * len(pairs) * rows * rows,
            transcendentals=0,
        ),
    )(*flat)


def products(gram, picks, blocks, base=None, tail=None):
    rows = gram.shape[1]
    tile = rows // 2 if rows % 32 == 0 else rows
    flat = [x for block in blocks for x in block]
    cut = blocks[0][0].shape[1]
    width = cut + blocks[0][1].shape[1]
    n = len(blocks)
    by_rows = pl.BlockSpec((tile, width), lambda m: (m, 0))
    specs = [pl.BlockSpec((gram.shape[0], tile, rows), lambda m: (0, m, 0))] + [held(x) for x in flat]
    args = [gram, *flat]
    if base is not None:
        specs.append(by_rows)
        args.append(base)
    if tail is not None:
        specs += [by_rows, pl.BlockSpec(memory_space=pltpu.SMEM)]
        args += tail

    def kernel(g, *refs):
        x, rest, out = refs[: 2 * n], list(refs[2 * n : -1]), refs[-1]
        for k, columns in enumerate((slice(0, cut), slice(cut, width))):
            value = None if base is None else rest[0][:, columns]
            for j, pick in enumerate(picks):
                term = jnp.dot(g[pick], x[2 * j + k][...], preferred_element_type=jnp.float32)
                value = term if value is None else value + term
            if tail is not None:
                normed = rest[-2][:, columns] / rest[-1][0, 0]
                value = (1.5 * normed - 0.5 * value) * jnp.sqrt(jnp.float32(3 * FF_WIN))
            out[:, columns] = value

    return pl.pallas_call(
        kernel,
        grid=(rows // tile,),
        in_specs=specs,
        out_specs=by_rows,
        out_shape=jax.ShapeDtypeStruct((rows, width), jnp.float32),
        cost_estimate=pl.CostEstimate(
            flops=2 * n * rows * rows * width,
            bytes_accessed=2 * n * rows * (rows + width) + 4 * rows * width,
            transcendentals=0,
        ),
    )(*args)


def scatter_sum(parts, me, n):
    for bit in bits_of(n):
        rows = parts.shape[1] // 2
        high = (me & bit) // bit
        take = lambda which: lax.dynamic_slice_in_dim(parts, which * rows, rows, 1)
        got = flip(take(1 - high), bit, n, "col")
        parts = take(high) + got
    return parts.astype(jnp.bfloat16)


def gather_rows(parts, me, n):
    for bit in reversed(bits_of(n)):
        other = flip(parts, bit, n, "col")
        low = (me & bit) == 0
        parts = jnp.concatenate([jnp.where(low, parts, other), jnp.where(low, other, parts)], 1)
    return parts


def solution(mesh):
    rows, cols = mesh.shape["row"], mesh.shape["col"]
    order = cycle(mesh)
    ahead = [(order[i], order[(i + 1) % rows]) for i in range(rows)]
    back = [(b, a) for a, b in ahead]
    far = rows // 2
    near = far // 2
    moved = lambda by: [(order[i], order[(i + by) % rows]) for i in range(rows)]

    def step_of(momentum, gradient):
        new_momentum = 0.95 * momentum + gradient
        squares = total(total(jnp.sum(new_momentum * new_momentum), "col", cols), "row", rows)
        norm = jnp.sqrt(3.0 * squares / D) + 1e-07
        normed = new_momentum / norm
        me = lax.axis_index("col")
        half = -(-normed.shape[1] // 256) * 128
        own = (normed[:, :half].astype(jnp.bfloat16), normed[:, half:].astype(jnp.bfloat16))
        blocks = {0: own}
        for d in range(1, far):
            for side, ring in ((-d, ahead), (d, back)):
                last = blocks[side + 1 if side < 0 else side - 1]
                got = []
                for k in (0, 1):
                    got.append(lax.ppermute(last[k], "row", ring))
                blocks[side] = tuple(got)
        last_a = lax.ppermute(blocks[1 - far][0], "row", ahead)
        last_b = lax.ppermute(blocks[far - 1][1], "row", back)
        blocks[far] = (last_a, last_b)

        crossing = [
            ((-(near - 1), near), -(near - 1), far - 1),
            ((near - 1, -near), near - 1, 1 - far),
            ((-near, near), -near, far),
        ]
        direct = {1: [0, -1, 1]} | {d: [-d, d] for d in range(2, far - 1)}
        shares = {}
        for d, js in direct.items():
            if d == near:
                shares["x"] = scatter_sum(grams([(blocks[i], blocks[j]) for (i, j), _, _ in crossing]), me, cols)
            shares[d] = scatter_sum(grams([(own, blocks[j]) for j in js]), me, cols)
        crossed = []
        for i, (_, by, j) in enumerate(crossing):
            crossed.append(lax.ppermute(shares["x"][i : i + 1], "row", moved(by)))
        total_so_far = None
        for d, js in direct.items():
            gram = gather_rows(shares[d], me, cols)
            total_so_far = products(gram, range(len(js)), [blocks[j] for j in js], total_so_far)
        gram = gather_rows(jnp.concatenate(crossed, 0), me, cols)
        total_so_far = products(gram, (0, 1), [blocks[far - 1], blocks[1 - far]], total_so_far)
        update = products(gram, (2,), [blocks[far]], total_so_far, (new_momentum, norm.reshape(1, 1)))
        return (new_momentum, update)

    placed = (P("row", "col"), P("row", "col"))
    return jax.shard_map(step_of, mesh=mesh, in_specs=placed, out_specs=placed, check_vma=False)
```

time: 937 us -> 491 us (0.52)
  waiting for transfers between devices: 796 us -> 275 us
  Pallas kernels: 0 us -> 108 us
  matrix products: 62.3 us -> 0 us
  starting transfers between devices: 0.12 us -> 43.8 us
  blocking collectives: 42.2 us -> 0 us
  other arithmetic: 21.3 us -> 38.5 us
  local copies, waits for them, and re-layouts: 0 us -> 12.1 us
  between operations: 14.4 us -> 4.49 us
    all_gather x2 -> x0, waiting for transfers between devices: 696 us -> none  [the longest x1 648 us: shards(): gathered = lax.all_gather(rounded, 'row', axis=0, tiled=True)]
    ppermute x0 -> x34, waiting for transfers between devices: none -> 275 us  [the longest x12 162 us: step_of(): got.append(lax.ppermute(last[k], 'row', ring))]
    pallas_call x0 -> x7, Pallas kernels: none -> 108 us  [the longest x4 58.8 us: products(): pl.pallas_call(kernel, grid=(rows // tile,), in_specs=specs, out_specs=by...]
    reduce_scatter x1 -> x0, waiting for transfers between devices: 101 us -> none  [shards(): lax.psum_scatter(partial_value, 'col', scatter_dimension=1, tiled=True)]
    dot_general x2 -> x0, matrix products: 62.3 us -> none  [the longest x1 33.1 us: shards(): jnp.dot(gram_rounded, gathered, preferred_element_type=jnp.float32)]
    ppermute x0 -> x34, starting transfers between devices: none -> 43.8 us  [the longest x17 24.7 us: flip(): return lax.ppermute(x, axis, [(i, i ^ bit) for i in range(n)])]
    psum x1 -> x0, blocking collectives: 42.2 us -> none  [shards(): squares = lax.psum(jnp.sum(new_momentum * new_momentum), ('row', 'col'))]
    dynamic_slice x0 -> x6, local copies, waits for them, and re-layouts: none -> 11.2 us  [scatter_sum(): take = lambda which: lax.dynamic_slice_in_dim(parts, which * rows, rows, 1)]
  transfers between devices with their start and end apart: 3 -> 34, of which waited for: 3 -> 21; matrix products, arithmetic and copies ran while one was open for 0% -> 7% of each run, Pallas kernels for 0% -> 20%
where the time goes in v1:
time: 491 us; the launch traced here: 482 us
  waiting for transfers between devices  275 us (56%)
  Pallas kernels  108 us (22%)
  starting transfers between devices  43.8 us (9%)
  other arithmetic  38.5 us (8%)
  local copies, waits for them, and re-layouts  12.1 us (2%)
    ppermute x12, waiting for transfers between devices, step_of(): got.append(lax.ppermute(last[k], 'row', ring))  162 us
    ppermute x17, waiting for transfers between devices, flip(): return lax.ppermute(x, axis, [(i, i ^ bit) for i in range(n)])  79.4 us
    pallas_call x4, Pallas kernels, products(): pl.pallas_call(kernel, grid=(rows // tile,), in_specs=specs, out_specs=by...  58.8 us
    pallas_call x3, Pallas kernels, grams(): pl.pallas_call(kernel, grid=(len(pairs),), in_specs=[held(x) for x in fla...  49.1 us
    ppermute x1, waiting for transfers between devices, step_of(): last_a = lax.ppermute(blocks[1 - far][0], 'row', ahead)  30.5 us
    ppermute x17, starting transfers between devices, flip(): return lax.ppermute(x, axis, [(i, i ^ bit) for i in range(n)])  24.7 us
    ppermute x12, starting transfers between devices, step_of(): got.append(lax.ppermute(last[k], 'row', ring))  12.3 us
    reduce_sum x1, other arithmetic, step_of(): jnp.sum(new_momentum * new_momentum)  12 us
  transfers between devices with their start and end apart: 34, of which 21 were waited for; matrix products, arithmetic and copies ran while one was open for 7% of the time, Pallas kernels for 20%

profile of v1, /device:TPU:0, one launch (start us, length us, event | category | flops | bytes accessed | tf_op | source)
XLA Modules:
  0.0 482.3 jit_solution(17660669340781239725)
XLA Ops:
  0.6 12.0 %multiply_reduce_fusion = (f32[]{:T(128)}, f32[640,3328]{1,0:T(8,128)}) fusion(f32[640,3328]{1,0:T(8,128)} %param.3, f32[640,3328]{1,0:T(8,128)} %param.2), kind=kLoop, calls=%fused_computation.1 | loop fusion | flops 8519679 | bytes 25559044 | tf_op jit(solution)/shard_map/reduce_sum | solution.py:159
  15.4 4.2 collective-permute-start.1
  20.5 3.4 collective-permute-start.2
  24.8 3.4 collective-permute-start.3
  29.2 4.4 collective-permute-start.4
  34.5 4.0 divide_convert_fusion
  43.0 45.3 %collective-permute-done.9.refs_5_ = bf16[640,1664]{1,0:T(8,128)(2,1)} collective-permute-done((bf16[640,1664]{1,0:T(8,128)(2,1)S(1)}, bf16[640,1664]{1,0:T(8,128)(2,1)}, u32[]{:S(2)}, u32[]{:S(2)}) %collective-permute-start.9) | collective-permute-done | bytes 2129952 | tf_op jit(solution)/shard_map/ppermute | solution.py:171
  90.3 45.5 %collective-permute-done.6.refs_1_.refs_3_ = bf16[640,1664]{1,0:T(8,128)(2,1)} collective-permute-done((bf16[640,1664]{1,0:T(8,128)(2,1)S(1)}, bf16[640,1664]{1,0:T(8,128)(2,1)}, u32[]{:S(2)}, u32[]{:S(2)}) %collective-permute-start.6) | collective-permute-done | bytes 2129952 | tf_op jit(solution)/shard_map/ppermute | solution.py:171
  137.8 17.0 %shard_map.43 = f32[3,640,640]{2,1,0:T(8,128)} custom-call(bf16[640,1664]{1,0:T(8,128)(2,1)} %copy-done.6, bf16[640,1664]{1,0:T(8,128)(2,1)} %copy-done.5, bf16[640,1664]{1,0:T(8,128)(2,1)} %collective-permute-done.5.refs_0_.refs_2_, bf16[640,1664]{1,0:T(8,128)(2,1)} %collective-permute-done.6.refs_1_.refs_3_, ...), custom_call_target="tpu_custom_call" | custom-call | flops 8178892800 | bytes 17694720 | tf_op jit(solution)/shard_map/pallas_call | solution.py:73
  156.8 22.8 %collective-permute-done.10.refs_3_.refs_5_ = bf16[640,1664]{1,0:T(8,128)(2,1)} collective-permute-done((bf16[640,1664]{1,0:T(8,128)(2,1)}, bf16[640,1664]{1,0:T(8,128)(2,1)}, u32[]{:S(2)}, u32[]{:S(2)}) %collective-permute-start.10) | collective-permute-done | bytes 2129952 | tf_op jit(solution)/shard_map/ppermute | solution.py:171
  181.4 39.4 %collective-permute-done.12.refs_7_.refs_3_.refs_1_ = bf16[640,1664]{1,0:T(8,128)(2,1)} collective-permute-done((bf16[640,1664]{1,0:T(8,128)(2,1)}, bf16[640,1664]{1,0:T(8,128)(2,1)}, u32[]{:S(2)}, u32[]{:S(2)}) %collective-permute-start.12) | collective-permute-done | bytes 2129952 | tf_op jit(solution)/shard_map/ppermute | solution.py:171
  220.8 18.7 %shard_map.41 = f32[3,640,640]{2,1,0:T(8,128)} custom-call(bf16[640,1664]{1,0:T(8,128)(2,1)} %collective-permute-done.5.refs_0_.refs_2_, bf16[640,1664]{1,0:T(8,128)(2,1)} %collective-permute-done.6.refs_1_.refs_3_, bf16[640,1664]{1,0:T(8,128)(2,1)} %collective-permute-done.8.refs_2_.refs_4_, bf16[640,1664]{1,0:T(8,128)(2,1)} %collective-permute-done.10.refs_3_.refs_5_, ...), custom_call_target="tpu_custom_call" | custom-call | flops 8178892800 | bytes 21954560 | tf_op jit(solution)/shard_map/pallas_call | solution.py:73
  239.5 3.3 constant_dynamic-slice_fusion.5
  242.7 13.5 %shard_map.42 = f32[2,640,640]{2,1,0:T(8,128)} custom-call(bf16[640,1664]{1,0:T(8,128)(2,1)} %copy-done.6, bf16[640,1664]{1,0:T(8,128)(2,1)} %copy-done.5, bf16[640,1664]{1,0:T(8,128)(2,1)} %collective-permute-done.11.refs_6_.refs_2_.refs_0_, bf16[640,1664]{1,0:T(8,128)(2,1)} %collective-permute-done.12.refs_7_.refs_3_.refs_1_, ...), custom_call_target="tpu_custom_call" | custom-call | flops 5452595200 | bytes 16056320 | tf_op jit(solution)/shard_map/pallas_call | solution.py:73
  256.2 2.7 constant_dynamic-slice_fusion.3
  259.4 2.7 dynamic-slice_add_fusion
  264.7 2.8 dynamic-slice_add_fusion.1
  276.0 17.4 %collective-permute-done.31 = f32[3,160,640]{2,1,0:T(8,128)} collective-permute-done((f32[3,160,640]{2,1,0:T(8,128)}, f32[3,160,640]{2,1,0:T(8,128)}, u32[]{:S(2)}, u32[]{:S(2)}) %collective-permute-start.31) | collective-permute-done | bytes 1228832 | tf_op jit(solution)/shard_map/ppermute | solution.py:32
  296.4 23.3 %collective-permute-done.14 = f32[3,160,640]{2,1,0:T(8,128)} collective-permute-done((f32[3,160,640]{2,1,0:T(8,128)}, f32[3,160,640]{2,1,0:T(8,128)}, u32[]{:S(2)}, u32[]{:S(2)}) %collective-permute-start.14) | collective-permute-done | bytes 1228832 | tf_op jit(solution)/shard_map/ppermute | solution.py:32
  322.9 14.3 %collective-permute-done.27 = f32[2,160,640]{2,1,0:T(8,128)S(1)} collective-permute-done((f32[2,160,640]{2,1,0:T(8,128)}, f32[2,160,640]{2,1,0:T(8,128)S(1)}, u32[]{:S(2)}, u32[]{:S(2)}) %collective-permute-start.27) | collective-permute-done | bytes 819232 | tf_op jit(solution)/shard_map/ppermute | solution.py:32
  337.7 2.7 collective-permute-start.17
  347.2 3.2 collective-permute-done.32
  351.6 7.5 %collective-permute-done.28 = bf16[2,160,640]{2,1,0:T(8,128)(2,1)S(1)} collective-permute-done((bf16[2,160,640]{2,1,0:T(8,128)(2,1)S(1)}, bf16[2,160,640]{2,1,0:T(8,128)(2,1)S(1)}, u32[]{:S(2)}, u32[]{:S(2)}) %collective-permute-start.28) | collective-permute-done | bytes 409632 | tf_op jit(solution)/shard_map/ppermute | solution.py:32
  360.2 11.1 %collective-permute-done.18 = bf16[3,160,640]{2,1,0:T(8,128)(2,1)S(1)} collective-permute-done((bf16[3,160,640]{2,1,0:T(8,128)(2,1)S(1)}, bf16[3,160,640]{2,1,0:T(8,128)(2,1)S(1)}, u32[]{:S(2)}, u32[]{:S(2)}) %collective-permute-start.18) | collective-permute-done | bytes 614432 | tf_op jit(solution)/shard_map/ppermute | solution.py:32
  379.5 2.7 broadcast_select_fusion.1
  385.5 18.1 %shard_map.44.refs_4_ = f32[640,3328]{1,0:T(8,128)} custom-call(bf16[3,640,640]{2,1,0:T(8,128)(2,1)} %pad_maximum_fusion.1.g, bf16[640,1664]{1,0:T(8,128)(2,1)} %copy-done.6, bf16[640,1664]{1,0:T(8,128)(2,1)} %copy-done.5, bf16[640,1664]{1,0:T(8,128)(2,1)} %collective-permute-done.5.refs_0_.refs_2_, ...), custom_call_target="tpu_custom_call" | custom-call | flops 8178892800 | bytes 23756800 | tf_op jit(solution)/shard_map/pallas_call | solution.py:116
  403.7 14.3 %shard_map.45.refs_4_ = f32[640,3328]{1,0:T(8,128)} custom-call(bf16[2,640,640]{2,1,0:T(8,128)(2,1)} %pad_maximum_fusion.2.g, bf16[640,1664]{1,0:T(8,128)(2,1)} %collective-permute-done.11.refs_6_.refs_2_.refs_0_, bf16[640,1664]{1,0:T(8,128)(2,1)} %collective-permute-done.12.refs_7_.refs_3_.refs_1_, ...), custom_call_target="tpu_custom_call" | custom-call | flops 5452595200 | bytes 18677760 | tf_op jit(solution)/shard_map/pallas_call | solution.py:116
  418.0 4.2 collective-permute-done.24.refs_0_
  422.1 3.1 collective-permute-done.25.refs_3_
  425.2 14.4 %shard_map.46.refs_2_ = f32[640,3328]{1,0:T(8,128)} custom-call(bf16[3,640,640]{2,1,0:T(8,128)(2,1)} %pad_maximum_fusion.g, bf16[640,1664]{1,0:T(8,128)(2,1)} %collective-permute-done.24.refs_0_, bf16[640,1664]{1,0:T(8,128)(2,1)} %collective-permute-done.22.refs_1_, bf16[640,1664]{1,0:T(8,128)(2,1)} %collective-permute-done.20.refs_2_, ...), custom_call_target="tpu_custom_call" | custom-call | flops 5452595200 | bytes 18677760 | tf_op jit(solution)/shard_map/pallas_call | solution.py:116
  439.7 30.5 %collective-permute-done.21.refs_0_ = bf16[640,1664]{1,0:T(8,128)(2,1)} collective-permute-done((bf16[640,1664]{1,0:T(8,128)(2,1)}, bf16[640,1664]{1,0:T(8,128)(2,1)}, u32[]{:S(2)}, u32[]{:S(2)}) %collective-permute-start.21) | collective-permute-done | bytes 2129952 | tf_op jit(solution)/shard_map/ppermute | solution.py:173
  470.1 11.9 %shard_map.47 = f32[640,3328]{1,0:T(8,128)} custom-call(bf16[3,640,640]{2,1,0:T(8,128)(2,1)} %pad_maximum_fusion.g, bf16[640,1664]{1,0:T(8,128)(2,1)} %collective-permute-done.21.refs_0_, bf16[640,1664]{1,0:T(8,128)(2,1)} %collective-permute-done.23.refs_1_, f32[640,3328]{1,0:T(8,128)} %shard_map.46.refs_2_, f32[640,3328]{1,0:T(8,128)} %get-tuple-element.3.refs_3_, ...), custom_call_target="tpu_custom_call" | custom-call | flops 2726297600 | bytes 13598720 | tf_op jit(solution)/shard_map/pallas_call | solution.py:116
  (87 shorter events, 54.1 us)
Async XLA Ops:
  15.4 4.6 collective-permute-start.1
  24.8 3.8 collective-permute-start.3
  29.2 4.8 collective-permute-start.4
  38.9 49.4 %collective-permute-start.9 = (bf16[640,1664]{1,0:T(8,128)(2,1)S(1)}, bf16[640,1664]{1,0:T(8,128)(2,1)}, u32[]{:S(2)}, u32[]{:S(2)}) collective-permute-start(bf16[640,1664]{1,0:T(8,128)(2,1)S(1)} %get-tuple-element.4.refs_1_), channel_id=1, source_target_pairs={{12,4},{20,12},{28,20},{24,28},{16,24},{8,16},{0,8},{4,0},{13,5},{... | collective-permute-start | bytes 6389768 | tf_op jit(solution)/shard_map/ppermute | solution.py:171
  40.8 49.3 %collective-permute-start.5 = (bf16[640,1664]{1,0:T(8,128)(2,1)S(1)}, bf16[640,1664]{1,0:T(8,128)(2,1)}, u32[]{:S(2)}, u32[]{:S(2)}) collective-permute-start(bf16[640,1664]{1,0:T(8,128)(2,1)S(1)} %get-tuple-element.5.refs_0_), channel_id=1, source_target_pairs={{4,12},{12,20},{20,28},{28,24},{24,16},{16,8},{8,0},{0,4},{5,13},{... | collective-permute-start | bytes 6389768 | tf_op jit(solution)/shard_map/ppermute | solution.py:171
  41.0 94.8 %collective-permute-start.6 = (bf16[640,1664]{1,0:T(8,128)(2,1)S(1)}, bf16[640,1664]{1,0:T(8,128)(2,1)}, u32[]{:S(2)}, u32[]{:S(2)}) collective-permute-start(bf16[640,1664]{1,0:T(8,128)(2,1)S(1)} %get-tuple-element.4.refs_1_), channel_id=1, source_target_pairs={{4,12},{12,20},{20,28},{28,24},{24,16},{16,8},{8,0},{0,4},{5,13},{... | collective-permute-start | bytes 6389768 | tf_op jit(solution)/shard_map/ppermute | solution.py:171
  42.8 93.1 %collective-permute-start.7 = (bf16[640,1664]{1,0:T(8,128)(2,1)S(1)}, bf16[640,1664]{1,0:T(8,128)(2,1)}, u32[]{:S(2)}, u32[]{:S(2)}) collective-permute-start(bf16[640,1664]{1,0:T(8,128)(2,1)S(1)} %get-tuple-element.5.refs_0_), channel_id=1, source_target_pairs={{12,4},{20,12},{28,20},{24,28},{16,24},{8,16},{0,8},{4,0},{13,5},{... | collective-permute-start | bytes 6389768 | tf_op jit(solution)/shard_map/ppermute | solution.py:171
  88.2 91.3 %collective-permute-start.10 = (bf16[640,1664]{1,0:T(8,128)(2,1)}, bf16[640,1664]{1,0:T(8,128)(2,1)}, u32[]{:S(2)}, u32[]{:S(2)}) collective-permute-start(bf16[640,1664]{1,0:T(8,128)(2,1)} %collective-permute-done.9.refs_5_), channel_id=1, source_target_pairs={{12,4},{20,12},{28,20},{24,28},{16,24},{8,16},{0,8},{4,0},{13,5},{... | collective-permute-start | bytes 6389768 | tf_op jit(solution)/shard_map/ppermute | solution.py:171
  90.2 91.3 %collective-permute-start.11 = (bf16[640,1664]{1,0:T(8,128)(2,1)}, bf16[640,1664]{1,0:T(8,128)(2,1)}, u32[]{:S(2)}, u32[]{:S(2)}) collective-permute-start(bf16[640,1664]{1,0:T(8,128)(2,1)} %collective-permute-done.5.refs_0_.refs_2_), channel_id=1, source_target_pairs={{4,12},{12,20},{20,28},{28,24},{24,16},{16,8},{8,0},{0,4},{5,13},{... | collective-permute-start | bytes 6389768 | tf_op jit(solution)/shard_map/ppermute | solution.py:171
  135.8 85.0 %collective-permute-start.12 = (bf16[640,1664]{1,0:T(8,128)(2,1)}, bf16[640,1664]{1,0:T(8,128)(2,1)}, u32[]{:S(2)}, u32[]{:S(2)}) collective-permute-start(bf16[640,1664]{1,0:T(8,128)(2,1)} %collective-permute-done.6.refs_1_.refs_3_), channel_id=1, source_target_pairs={{4,12},{12,20},{20,28},{28,24},{24,16},{16,8},{8,0},{0,4},{5,13},{... | collective-permute-start | bytes 6389768 | tf_op jit(solution)/shard_map/ppermute | solution.py:171
  135.9 84.9 %collective-permute-start.8 = (bf16[640,1664]{1,0:T(8,128)(2,1)}, bf16[640,1664]{1,0:T(8,128)(2,1)}, u32[]{:S(2)}, u32[]{:S(2)}) collective-permute-start(bf16[640,1664]{1,0:T(8,128)(2,1)} %collective-permute-done.7.refs_4_), channel_id=1, source_target_pairs={{12,4},{20,12},{28,20},{24,28},{16,24},{8,16},{0,8},{4,0},{13,5},{... | collective-permute-start | bytes 6389768 | tf_op jit(solution)/shard_map/ppermute | solution.py:171
  156.7 102.7 %collective-permute-start.30 = (f32[3,320,640]{2,1,0:T(8,128)S(1)}, f32[3,320,640]{2,1,0:T(8,128)}, u32[]{:S(2)}, u32[]{:S(2)}) collective-permute-start(f32[3,320,640]{2,1,0:T(8,128)S(1)} %constant_dynamic-slice_fusion.1), channel_id=1, source_target_pairs={{0,1},{1,0},{2,3},{3,2},{4,5},{5,4},{6,7},{7,6},{8,9},{9,8},{10,11... | collective-permute-start | bytes 7372808 | tf_op jit(solution)/shard_map/ppermute | solution.py:32
  242.7 22.0 %collective-permute-start.13 = (f32[3,320,640]{2,1,0:T(8,128)}, f32[3,320,640]{2,1,0:T(8,128)}, u32[]{:S(2)}, u32[]{:S(2)}) collective-permute-start(f32[3,320,640]{2,1,0:T(8,128)} %constant_dynamic-slice_fusion.5), channel_id=1, source_target_pairs={{0,1},{1,0},{2,3},{3,2},{4,5},{5,4},{6,7},{7,6},{8,9},{9,8},{10,11... | collective-permute-start | bytes 7372808 | tf_op jit(solution)/shard_map/ppermute | solution.py:32
  258.9 10.4 %collective-permute-start.26 = (f32[2,320,640]{2,1,0:T(8,128)}, f32[2,320,640]{2,1,0:T(8,128)}, u32[]{:S(2)}, u32[]{:S(2)}) collective-permute-start(f32[2,320,640]{2,1,0:T(8,128)} %constant_dynamic-slice_fusion.3), channel_id=1, source_target_pairs={{0,1},{1,0},{2,3},{3,2},{4,5},{5,4},{6,7},{7,6},{8,9},{9,8},{10,11... | collective-permute-start | bytes 4915208 | tf_op jit(solution)/shard_map/ppermute | solution.py:32
  263.2 30.2 %collective-permute-start.31 = (f32[3,160,640]{2,1,0:T(8,128)}, f32[3,160,640]{2,1,0:T(8,128)}, u32[]{:S(2)}, u32[]{:S(2)}) collective-permute-start(f32[3,160,640]{2,1,0:T(8,128)} %constant_dynamic-slice_fusion), channel_id=1, source_target_pairs={{0,2},{1,3},{2,0},{3,1},{4,6},{5,7},{6,4},{7,5},{8,10},{9,11},{10,... | collective-permute-start | bytes 3686408 | tf_op jit(solution)/shard_map/ppermute | solution.py:32
  268.8 50.9 %collective-permute-start.14 = (f32[3,160,640]{2,1,0:T(8,128)}, f32[3,160,640]{2,1,0:T(8,128)}, u32[]{:S(2)}, u32[]{:S(2)}) collective-permute-start(f32[3,160,640]{2,1,0:T(8,128)} %constant_dynamic-slice_fusion.4), channel_id=1, source_target_pairs={{0,2},{1,3},{2,0},{3,1},{4,6},{5,7},{6,4},{7,5},{8,10},{9,11},{10,... | collective-permute-start | bytes 3686408 | tf_op jit(solution)/shard_map/ppermute | solution.py:32
  272.5 64.7 %collective-permute-start.27 = (f32[2,160,640]{2,1,0:T(8,128)}, f32[2,160,640]{2,1,0:T(8,128)S(1)}, u32[]{:S(2)}, u32[]{:S(2)}) collective-permute-start(f32[2,160,640]{2,1,0:T(8,128)} %constant_dynamic-slice_fusion.2), channel_id=1, source_target_pairs={{0,2},{1,3},{2,0},{3,1},{4,6},{5,7},{6,4},{7,5},{8,10},{9,11},{10,... | collective-permute-start | bytes 2457608 | tf_op jit(solution)/shard_map/ppermute | solution.py:32
  274.0 101.7 %collective-permute-start.20 = (bf16[640,1664]{1,0:T(8,128)(2,1)}, bf16[640,1664]{1,0:T(8,128)(2,1)}, u32[]{:S(2)}, u32[]{:S(2)}) collective-permute-start(bf16[640,1664]{1,0:T(8,128)(2,1)} %collective-permute-done.11.refs_6_.refs_2_.refs_0_), channel_id=1, source_target_pairs={{4,12},{12,20},{20,28},{28,24},{24,16},{16,8},{8,0},{0,4},{5,13},{... | collective-permute-start | bytes 6389768 | tf_op jit(solution)/shard_map/ppermute | solution.py:171
  274.4 103.0 %collective-permute-start.22 = (bf16[640,1664]{1,0:T(8,128)(2,1)}, bf16[640,1664]{1,0:T(8,128)(2,1)}, u32[]{:S(2)}, u32[]{:S(2)}) collective-permute-start(bf16[640,1664]{1,0:T(8,128)(2,1)} %collective-permute-done.10.refs_3_.refs_5_), channel_id=1, source_target_pairs={{12,4},{20,12},{28,20},{24,28},{16,24},{8,16},{0,8},{4,0},{13,5},{... | collective-permute-start | bytes 6389768 | tf_op jit(solution)/shard_map/ppermute | solution.py:171
  294.8 55.5 %collective-permute-start.32 = (bf16[3,160,640]{2,1,0:T(8,128)(2,1)S(1)}, bf16[3,160,640]{2,1,0:T(8,128)(2,1)S(1)}, u32[]{:S(2)}, u32[]{:S(2)}) collective-permute-start(bf16[3,160,640]{2,1,0:T(8,128)(2,1)S(1)} %add_convert_fusion), channel_id=1, source_target_pairs={{0,2},{1,3},{2,0},{3,1},{4,6},{5,7},{6,4},{7,5},{8,10},{9,11},{10,... | collective-permute-start | bytes 1843208 | tf_op jit(solution)/shard_map/ppermute | solution.py:32
  321.3 16.4 %collective-permute-start.15 = (bf16[1,160,640]{2,1,0:T(8,128)(2,1)S(1)}, bf16[1,160,640]{2,1,0:T(8,128)(2,1)S(1)}, u32[]{:S(2)}, u32[]{:S(2)}) collective-permute-start(bf16[1,160,640]{2,1,0:T(8,128)(2,1)S(1)} %get-tuple-element.20), channel_id=1, source_target_pairs={{4,0},{12,4},{20,12},{28,20},{24,28},{16,24},{8,16},{0,8},{5,1},{1... | collective-permute-start | bytes 614408 | tf_op jit(solution)/shard_map/ppermute | solution.py:190
  337.2 5.8 %collective-permute-start.16 = (bf16[1,160,640]{2,1,0:T(8,128)(2,1)S(1)}, bf16[1,160,640]{2,1,0:T(8,128)(2,1)S(1)}, u32[]{:S(2)}, u32[]{:S(2)}) collective-permute-start(bf16[1,160,640]{2,1,0:T(8,128)(2,1)S(1)} %get-tuple-element.19), channel_id=1, source_target_pairs={{4,12},{12,20},{20,28},{28,24},{24,16},{16,8},{8,0},{0,4},{5,13},{... | collective-permute-start | bytes 614408 | tf_op jit(solution)/shard_map/ppermute | solution.py:190
  337.7 7.8 %collective-permute-start.17 = (bf16[1,160,640]{2,1,0:T(8,128)(2,1)S(1)}, bf16[1,160,640]{2,1,0:T(8,128)(2,1)S(1)}, u32[]{:S(2)}, u32[]{:S(2)}) collective-permute-start(bf16[1,160,640]{2,1,0:T(8,128)(2,1)S(1)} %get-tuple-element.18), channel_id=1, source_target_pairs={{4,8},{12,0},{20,4},{28,12},{24,20},{16,28},{8,24},{0,16},{5,9},{1... | collective-permute-start | bytes 614408 | tf_op jit(solution)/shard_map/ppermute | solution.py:190
  343.0 16.2 %collective-permute-start.28 = (bf16[2,160,640]{2,1,0:T(8,128)(2,1)S(1)}, bf16[2,160,640]{2,1,0:T(8,128)(2,1)S(1)}, u32[]{:S(2)}, u32[]{:S(2)}) collective-permute-start(bf16[2,160,640]{2,1,0:T(8,128)(2,1)S(1)} %add_convert_fusion.2), channel_id=1, source_target_pairs={{0,2},{1,3},{2,0},{3,1},{4,6},{5,7},{6,4},{7,5},{8,10},{9,11},{10,... | collective-permute-start | bytes 1228808 | tf_op jit(solution)/shard_map/ppermute | solution.py:32
  345.5 25.8 %collective-permute-start.18 = (bf16[3,160,640]{2,1,0:T(8,128)(2,1)S(1)}, bf16[3,160,640]{2,1,0:T(8,128)(2,1)S(1)}, u32[]{:S(2)}, u32[]{:S(2)}) collective-permute-start(bf16[3,160,640]{2,1,0:T(8,128)(2,1)S(1)} %constant_dynamic-update-slice_fusion), channel_id=1, source_target_pairs={{0,2},{1,3},{2,0},{3,1},{4,6},{5,7},{6,4},{7,5},{8,10},{9,11},{10,... | collective-permute-start | bytes 1843208 | tf_op jit(solution)/shard_map/ppermute | solution.py:32
  351.6 26.3 %collective-permute-start.33 = (bf16[3,320,640]{2,1,0:T(8,128)(2,1)}, bf16[3,320,640]{2,1,0:T(8,128)(2,1)}, u32[]{:S(2)}, u32[]{:S(2)}) collective-permute-start(bf16[3,320,640]{2,1,0:T(8,128)(2,1)} %pad_maximum_fusion.4), channel_id=1, source_target_pairs={{0,1},{1,0},{2,3},{3,2},{4,5},{5,4},{6,7},{7,6},{8,9},{9,8},{10,11... | collective-permute-start | bytes 3686408 | tf_op jit(solution)/shard_map/ppermute | solution.py:32
  360.2 12.4 %collective-permute-start.29 = (bf16[2,320,640]{2,1,0:T(8,128)(2,1)}, bf16[2,320,640]{2,1,0:T(8,128)(2,1)}, u32[]{:S(2)}, u32[]{:S(2)}) collective-permute-start(bf16[2,320,640]{2,1,0:T(8,128)(2,1)} %pad_maximum_fusion.5), channel_id=1, source_target_pairs={{0,1},{1,0},{2,3},{3,2},{4,5},{5,4},{6,7},{7,6},{8,9},{9,8},{10,11... | collective-permute-start | bytes 2457608 | tf_op jit(solution)/shard_map/ppermute | solution.py:32
  372.6 6.9 %collective-permute-start.19 = (bf16[3,320,640]{2,1,0:T(8,128)(2,1)}, bf16[3,320,640]{2,1,0:T(8,128)(2,1)}, u32[]{:S(2)}, u32[]{:S(2)}) collective-permute-start(bf16[3,320,640]{2,1,0:T(8,128)(2,1)} %pad_maximum_fusion.3), channel_id=1, source_target_pairs={{0,1},{1,0},{2,3},{3,2},{4,5},{5,4},{6,7},{7,6},{8,9},{9,8},{10,11... | collective-permute-start | bytes 3686408 | tf_op jit(solution)/shard_map/ppermute | solution.py:32
  372.6 49.5 %collective-permute-start.24 = (bf16[640,1664]{1,0:T(8,128)(2,1)}, bf16[640,1664]{1,0:T(8,128)(2,1)}, u32[]{:S(2)}, u32[]{:S(2)}) collective-permute-start(bf16[640,1664]{1,0:T(8,128)(2,1)} %collective-permute-done.8.refs_2_.refs_4_), channel_id=1, source_target_pairs={{12,4},{20,12},{28,20},{24,28},{16,24},{8,16},{0,8},{4,0},{13,5},{... | collective-permute-start | bytes 6389768 | tf_op jit(solution)/shard_map/ppermute | solution.py:171
  375.7 49.6 %collective-permute-start.25 = (bf16[640,1664]{1,0:T(8,128)(2,1)}, bf16[640,1664]{1,0:T(8,128)(2,1)}, u32[]{:S(2)}, u32[]{:S(2)}) collective-permute-start(bf16[640,1664]{1,0:T(8,128)(2,1)} %collective-permute-done.12.refs_7_.refs_3_.refs_1_), channel_id=1, source_target_pairs={{4,12},{12,20},{20,28},{28,24},{24,16},{16,8},{8,0},{0,4},{5,13},{... | collective-permute-start | bytes 6389768 | tf_op jit(solution)/shard_map/ppermute | solution.py:171
  377.5 92.7 %collective-permute-start.21 = (bf16[640,1664]{1,0:T(8,128)(2,1)}, bf16[640,1664]{1,0:T(8,128)(2,1)}, u32[]{:S(2)}, u32[]{:S(2)}) collective-permute-start(bf16[640,1664]{1,0:T(8,128)(2,1)} %collective-permute-done.20.refs_2_), channel_id=1, source_target_pairs={{4,12},{12,20},{20,28},{28,24},{24,16},{16,8},{8,0},{0,4},{5,13},{... | collective-permute-start | bytes 6389768 | tf_op jit(solution)/shard_map/ppermute | solution.py:173
  377.9 92.3 %collective-permute-start.23 = (bf16[640,1664]{1,0:T(8,128)(2,1)}, bf16[640,1664]{1,0:T(8,128)(2,1)}, u32[]{:S(2)}, u32[]{:S(2)}) collective-permute-start(bf16[640,1664]{1,0:T(8,128)(2,1)} %collective-permute-done.22.refs_1_), channel_id=1, source_target_pairs={{12,4},{20,12},{28,20},{24,28},{16,24},{8,16},{0,8},{4,0},{13,5},{... | collective-permute-start | bytes 6389768 | tf_op jit(solution)/shard_map/ppermute | solution.py:174
  (9 other events, 299.2 us)

commit v2 on v1

v2 whole, which is shorter than its diff:
```python
import jax
import jax.numpy as jnp
from jax import lax
from jax.experimental import pallas as pl
from jax.experimental.pallas import tpu as pltpu
from jax.sharding import PartitionSpec as P


D = 5120
FF_WIN = 13312


def cycle(mesh):
    places = [tuple(d.coords) for d in mesh.devices[:, 0]]
    n = len(places)
    first = [a != b for a, b in zip(places[0], places[1 % n])]
    minor = n
    for i, place in enumerate(places):
        if any(a != b and not f for a, b, f in zip(place, places[0], first)):
            minor = i
            break
    major = n // minor
    order = []
    for i in range(major):
        along = range(1, minor) if i % 2 == 0 else range(minor - 1, 0, -1)
        order += [i * minor + j for j in along]
    order += [i * minor for i in range(major - 1, -1, -1)]
    return order


def flip(x, bit, n, axis):
    return lax.ppermute(x, axis, [(i, i ^ bit) for i in range(n)])


def bits_of(n):
    return [1 << k for k in range(n.bit_length() - 1)]


def total(x, axis, n):
    for bit in bits_of(n):
        x = x + flip(x, bit, n, axis)
    return x


def dot_rows(left, right):
    return lax.dot_general(left, right, (((1,), (1,)), ((), ())), preferred_element_type=jnp.float32)


def into(block, dst, sems):
    at, copies = 0, []
    for i, piece in enumerate(block):
        wide = piece.shape[1]
        copies.append(pltpu.make_async_copy(piece, dst.at[:, at : at + wide], sems.at[i]))
        at += wide
    return copies


ANY = pl.BlockSpec(memory_space=pl.ANY)


def grams(pairs, high):
    given = []
    for pair in pairs:
        for block in pair:
            if not any(block is g for g in given):
                given.append(block)
    at = lambda block: next(i for i, g in enumerate(given) if g is block)
    flat = [x for block in given for x in block]
    rows, half = flat[0].shape[0], flat[0].shape[0] // 2
    width = sum(x.shape[1] for x in given[0])
    same = all(left is pairs[0][0] for left, _ in pairs)

    def kernel(high_ref, *refs):
        kept, sent, left, right, sems = refs[len(flat) :]
        block = lambda b: refs[2 * at(b) : 2 * at(b) + 2]

        def copies(p):
            got = into(block(pairs[p][1]), right.at[p % 2], sems.at[p % 2, 0])
            if p == 0 or not same:
                got += into(block(pairs[p][0]), left.at[p % 2], sems.at[p % 2, 1])
            return got

        step = pl.program_id(0)
        for p in range(len(pairs)):

            @pl.when(step == p)
            def _():
                for q in (0, 1) if p == 0 else (p + 1,):
                    if q < len(pairs):
                        for c in copies(q):
                            c.start()
                for c in copies(p):
                    c.wait()

        slot = lax.rem(step, 2)
        value = dot_rows(left[0 if same else slot], right[slot])

        @pl.when(high_ref[0] == 0)
        def _():
            kept[0] = value[:half]
            sent[0] = value[half:]

        @pl.when(high_ref[0] != 0)
        def _():
            kept[0] = value[half:]
            sent[0] = value[:half]

    out = pl.BlockSpec((1, half, rows), lambda p: (p, 0, 0))
    return pl.pallas_call(
        kernel,
        grid=(len(pairs),),
        in_specs=[pl.BlockSpec(memory_space=pltpu.SMEM)] + [ANY] * len(flat),
        out_specs=(out, out),
        out_shape=(jax.ShapeDtypeStruct((len(pairs), half, rows), jnp.float32),) * 2,
        scratch_shapes=[
            pltpu.VMEM((1 if same else 2, rows, width), jnp.bfloat16),
            pltpu.VMEM((2, rows, width), jnp.bfloat16),
            pltpu.SemaphoreType.DMA((2, 2, 2)),
        ],
        cost_estimate=pl.CostEstimate(
            flops=2 * len(pairs) * rows * rows * width,
            bytes_accessed=2 * len(flat) * flat[0].size + 4 * len(pairs) * rows * rows,
            transcendentals=0,
        ),
    )(high.reshape(1), *flat)


def products(gram, picks, blocks, high, base=None, tail=None, scale=1.0, cuts=1):
    n = len(blocks)
    half, rows = gram[0].shape[1:]
    flat = [x for block in blocks for x in block]
    width = sum(x.shape[1] for x in blocks[0])
    cuts = cuts if half % (16 * cuts) == 0 else 1
    tile = half // cuts
    by_rows = pl.BlockSpec((tile, width), lambda m, hi: (cuts * ((m // cuts + hi[0]) % 2) + m % cuts, 0))
    specs = [ANY] * (2 + len(flat))
    args = [*gram, *flat]
    if base is not None:
        specs.append(by_rows)
        args.append(base)
    if tail is not None:
        specs += [by_rows, pl.BlockSpec(memory_space=pltpu.SMEM)]
        args += tail

    def kernel(_, mine, other, *refs):
        pieces, rest = refs[: 2 * n], refs[2 * n : -5]
        out, g, x, g_sems, x_sems = refs[-5:]
        m = pl.program_id(0)

        def copies(j):
            halves = [
                pltpu.make_async_copy(src.at[picks[j]], g.at[i, j], g_sems.at[i, j]) for i, src in enumerate((mine, other))
            ]
            return halves + into(pieces[2 * j : 2 * j + 2], x.at[j], x_sems.at[j])

        @pl.when(m == 0)
        def _():
            for j in range(n):
                for c in copies(j):
                    c.start()

        out[...] = jnp.zeros_like(out) if base is None else rest[0][...]

        def add(j, carry):
            for i in range(n):

                @pl.when((m == 0) & (j == i))
                def _():
                    for c in copies(i):
                        c.wait()

            here = pl.ds(pl.multiple_of(lax.rem(m, cuts) * tile, tile), tile)
            out[...] += scale * jnp.dot(g[m // cuts, j, here, :], x[j], preferred_element_type=jnp.float32)
            return carry

        lax.fori_loop(0, n, add, 0)
        if tail is not None:
            normed = rest[-2][...] / rest[-1][0, 0]
            out[...] = (1.5 * normed - 0.5 * out[...]) * jnp.sqrt(jnp.float32(3 * FF_WIN))

    return pl.pallas_call(
        kernel,
        grid_spec=pltpu.PrefetchScalarGridSpec(
            num_scalar_prefetch=1,
            grid=(2 * cuts,),
            in_specs=specs,
            out_specs=by_rows,
            scratch_shapes=[
                pltpu.VMEM((2, n, half, rows), jnp.bfloat16),
                pltpu.VMEM((n, rows, width), jnp.bfloat16),
                pltpu.SemaphoreType.DMA((2, n)),
                pltpu.SemaphoreType.DMA((n, 2)),
            ],
        ),
        out_shape=jax.ShapeDtypeStruct((rows, width), jnp.float32),
        cost_estimate=pl.CostEstimate(
            flops=2 * n * rows * rows * width,
            bytes_accessed=2 * n * rows * (rows + width) + 4 * rows * width,
            transcendentals=0,
        ),
    )(high.reshape(1), *args)


def scatter_sum(halves, me, n):
    kept, sent = halves
    for bit in bits_of(n):
        if bit > 1:
            rows = parts.shape[1] // 2
            high = (me & bit) // bit
            sent = lax.dynamic_slice_in_dim(parts, (1 - high) * rows, rows, 1)
            kept = lax.dynamic_slice_in_dim(parts, high * rows, rows, 1)
        parts = kept + flip(sent, bit, n, "col")
    return parts.astype(jnp.bfloat16)


def gather_rows(parts, me, n):
    for bit in reversed(bits_of(n)):
        other = flip(parts, bit, n, "col")
        if bit > 1:
            low = (me & bit) == 0
            parts = jnp.concatenate([jnp.where(low, parts, other), jnp.where(low, other, parts)], 1)
    return parts, other


def solution(mesh):
    rows, cols = mesh.shape["row"], mesh.shape["col"]
    order = cycle(mesh)
    ahead = [(order[i], order[(i + 1) % rows]) for i in range(rows)]
    back = [(b, a) for a, b in ahead]
    far = rows // 2
    near = far // 2
    moved = lambda by: [(order[i], order[(i + by) % rows]) for i in range(rows)]

    def step_of(momentum, gradient):
        new_momentum = 0.95 * momentum + gradient
        squares = total(total(jnp.sum(new_momentum * new_momentum), "col", cols), "row", rows)
        norm = jnp.sqrt(3.0 * squares / D) + 1e-07
        normed = new_momentum / norm
        me = lax.axis_index("col")
        high = (me & 1).astype(jnp.int32)
        half = -(-normed.shape[1] // 256) * 128
        own = (normed[:, :half].astype(jnp.bfloat16), normed[:, half:].astype(jnp.bfloat16))
        blocks = {0: own}
        for d in range(1, far):
            for side, ring in ((-d, ahead), (d, back)):
                last = blocks[side + 1 if side < 0 else side - 1]
                got = []
                for k in (0, 1):
                    got.append(lax.ppermute(last[k], "row", ring))
                blocks[side] = tuple(got)
        last_a = lax.ppermute(blocks[1 - far][0], "row", ahead)
        last_b = lax.ppermute(blocks[far - 1][1], "row", back)
        blocks[far] = (last_a, last_b)

        crossing = [
            ((-(near - 1), near), -(near - 1), far - 1),
            ((near - 1, -near), near - 1, 1 - far),
            ((-near, near), -near, far),
        ]
        direct = {1: [0, -1, 1]} | {d: [-d, d] for d in range(2, far - 1)}
        shares = {}
        for d, js in direct.items():
            shares[d] = scatter_sum(grams([(own, blocks[j]) for j in js], high), me, cols)
            if d == near:
                pairs = [(blocks[i], blocks[j]) for (i, j), _, _ in crossing]
                shares["x"] = scatter_sum(grams(pairs, high), me, cols)
        crossed = []
        for i, (_, by, j) in enumerate(crossing):
            crossed.append(lax.ppermute(shares["x"][i : i + 1], "row", moved(by)))
        totals = [None]
        for d, js in direct.items():
            gram = gather_rows(shares[d], me, cols)
            totals.append(products(gram, range(len(js)), [blocks[j] for j in js], high, totals[-1]))
        crossed, _ = lax.optimization_barrier((jnp.concatenate(crossed, 0), totals[1]))
        gram = gather_rows(crossed, me, cols)
        most = products(
            gram, (0, 1), [blocks[far - 1], blocks[1 - far]], high, totals[-1], (new_momentum, norm.reshape(1, 1))
        )
        scale = -0.5 * (3 * FF_WIN) ** 0.5
        update = products(gram, (2,), [blocks[far]], high, most, scale=scale, cuts=2)
        return (new_momentum, update)

    placed = (P("row", "col"), P("row", "col"))
    return jax.shard_map(step_of, mesh=mesh, in_specs=placed, out_specs=placed, check_vma=False)
```

time: 491 us -> 474 us (0.965); the launches traced: 482 us -> 473 us
  other arithmetic: 38.5 us -> 27.3 us
  waiting for transfers between devices: 275 us -> 286 us
  local copies, waits for them, and re-layouts: 12.1 us -> 6.01 us
    ppermute x12, waiting for transfers between devices: 162 us -> 175 us  [step_of(): got.append(lax.ppermute(last[k], 'row', ring))]
    ppermute x3, waiting for transfers between devices: 3.51 us -> 13.4 us  [step_of(): crossed.append(lax.ppermute(shares['x'][i:i + 1], 'row', moved(by)))]
    dynamic_slice x6 -> x3, local copies, waits for them, and re-layouts: 11.2 us -> 2.31 us  [scatter_sum(): sent = lax.dynamic_slice_in_dim(parts, (1 - high) * rows, rows, 1)]
    concatenate x6 -> x3, other arithmetic: 7.87 us -> 0.29 us  [gather_rows(): jnp.concatenate([jnp.where(low, parts, other), jnp.where(low, other, part...]
    ppermute x1, waiting for transfers between devices: 30.5 us -> 23 us  [step_of(): last_a = lax.ppermute(blocks[1 - far][0], 'row', ahead)]
  transfers between devices with their start and end apart: 34 -> 34, of which waited for: 21 -> 19; matrix products, arithmetic and copies ran while one was open for 7% -> 3% of each run, Pallas kernels for 20% -> 20%
where the time goes in v2:
time: 474 us; the launch traced here: 473 us
  waiting for transfers between devices  286 us (60%)
  Pallas kernels  106 us (22%)
  starting transfers between devices  43 us (9%)
  other arithmetic  27.3 us (6%)
  local copies, waits for them, and re-layouts  6.01 us (1%)
  between operations  5.05 us (1%)
    ppermute x12, waiting for transfers between devices, step_of(): got.append(lax.ppermute(last[k], 'row', ring))  175 us
    ppermute x17, waiting for transfers between devices, flip(): return lax.ppermute(x, axis, [(i, i ^ bit) for i in range(n)])  74.6 us
    pallas_call x4, Pallas kernels, products(): pl.pallas_call(kernel, grid_spec=pltpu.PrefetchScalarGridSpec(num_scalar_...  61.2 us
    pallas_call x3, Pallas kernels, grams(): pl.pallas_call(kernel, grid=(len(pairs),), in_specs=[pl.BlockSpec(memory_...  44.8 us
    ppermute x17, starting transfers between devices, flip(): return lax.ppermute(x, axis, [(i, i ^ bit) for i in range(n)])  23.8 us
    ppermute x1, waiting for transfers between devices, step_of(): last_a = lax.ppermute(blocks[1 - far][0], 'row', ahead)  23 us
    ppermute x3, waiting for transfers between devices, step_of(): crossed.append(lax.ppermute(shares['x'][i:i + 1], 'row', moved(by)))  13.4 us
    ppermute x12, starting transfers between devices, step_of(): got.append(lax.ppermute(last[k], 'row', ring))  12.3 us
  transfers between devices with their start and end apart: 34, of which 19 were waited for; matrix products, arithmetic and copies ran while one was open for 3% of the time, Pallas kernels for 20%

profile of v2, /device:TPU:0, one launch (start us, length us, event | category | flops | bytes accessed | tf_op | source)
XLA Modules:
  0.0 473.1 jit_solution(11598929404954296929)
XLA Ops:
  0.6 12.0 %multiply_reduce_fusion = (f32[]{:T(128)}, f32[640,3328]{1,0:T(8,128)}) fusion(f32[640,3328]{1,0:T(8,128)} %param.3, f32[640,3328]{1,0:T(8,128)} %param.2), kind=kLoop, calls=%fused_computation.1 | loop fusion | flops 8519679 | bytes 25559044 | tf_op jit(solution)/shard_map/reduce_sum | solution.py:236
  15.5 4.2 collective-permute-start.1
  20.7 3.4 collective-permute-start.2
  25.1 3.4 collective-permute-start.3
  29.5 4.4 collective-permute-start.4
  35.0 4.0 divide_convert_fusion
  39.3 2.0 collective-permute-start.9
  43.4 45.3 %collective-permute-done.9.refs_5_ = bf16[640,1664]{1,0:T(8,128)(2,1)} collective-permute-done((bf16[640,1664]{1,0:T(8,128)(2,1)S(1)}, bf16[640,1664]{1,0:T(8,128)(2,1)}, u32[]{:S(2)}, u32[]{:S(2)}) %collective-permute-start.9) | collective-permute-done | bytes 2129952 | tf_op jit(solution)/shard_map/ppermute | solution.py:249
  88.7 1.9 collective-permute-start.10
  90.7 45.5 %collective-permute-done.6.refs_1_.refs_3_ = bf16[640,1664]{1,0:T(8,128)(2,1)} collective-permute-done((bf16[640,1664]{1,0:T(8,128)(2,1)S(1)}, bf16[640,1664]{1,0:T(8,128)(2,1)}, u32[]{:S(2)}, u32[]{:S(2)}) %collective-permute-start.6) | collective-permute-done | bytes 2129952 | tf_op jit(solution)/shard_map/ppermute | solution.py:249
  136.4 1.9 collective-permute-start.8
  138.3 16.8 %shard_map.42 = (f32[3,320,640]{2,1,0:T(8,128)}, f32[3,320,640]{2,1,0:T(8,128)}) custom-call(s32[1]{0:T(128)} %bitcast.high_ref._, bf16[640,1664]{1,0:T(8,128)(2,1)} %copy-done.6, bf16[640,1664]{1,0:T(8,128)(2,1)} %copy-done.5, bf16[640,1664]{1,0:T(8,128)(2,1)} %collective-permute-done.5.refs_0_.refs_2_, ...), custom_call_target="tpu_custom_call" | custom-call | flops 8178892800 | bytes 17694720 | tf_op jit(solution)/shard_map/pallas_call | solution.py:109
  155.2 24.8 %collective-permute-done.10.refs_3_.refs_5_ = bf16[640,1664]{1,0:T(8,128)(2,1)} collective-permute-done((bf16[640,1664]{1,0:T(8,128)(2,1)}, bf16[640,1664]{1,0:T(8,128)(2,1)}, u32[]{:S(2)}, u32[]{:S(2)}) %collective-permute-start.10) | collective-permute-done | bytes 2129952 | tf_op jit(solution)/shard_map/ppermute | solution.py:249
  181.9 39.4 %collective-permute-done.12.refs_7_.refs_3_.refs_1_ = bf16[640,1664]{1,0:T(8,128)(2,1)} collective-permute-done((bf16[640,1664]{1,0:T(8,128)(2,1)}, bf16[640,1664]{1,0:T(8,128)(2,1)}, u32[]{:S(2)}, u32[]{:S(2)}) %collective-permute-start.12) | collective-permute-done | bytes 2129952 | tf_op jit(solution)/shard_map/ppermute | solution.py:249
  221.2 16.0 %shard_map.41 = (f32[3,320,640]{2,1,0:T(8,128)}, f32[3,320,640]{2,1,0:T(8,128)}) custom-call(s32[1]{0:T(128)} %bitcast.high_ref._, bf16[640,1664]{1,0:T(8,128)(2,1)} %collective-permute-done.5.refs_0_.refs_2_, bf16[640,1664]{1,0:T(8,128)(2,1)} %collective-permute-done.6.refs_1_.refs_3_, bf16[640,1664]{1,0:T(8,128)(2,1)} %collective-permute-done.8.refs_2_.refs_4_, ...), custom_call_target="tpu_custom_call" | custom-call | flops 8178892800 | bytes 21954560 | tf_op jit(solution)/shard_map/pallas_call | solution.py:109
  238.8 2.7 add.61
  244.1 12.0 %shard_map.44 = (f32[2,320,640]{2,1,0:T(8,128)}, f32[2,320,640]{2,1,0:T(8,128)}) custom-call(s32[1]{0:T(128)} %bitcast.high_ref._, bf16[640,1664]{1,0:T(8,128)(2,1)} %copy-done.6, bf16[640,1664]{1,0:T(8,128)(2,1)} %copy-done.5, bf16[640,1664]{1,0:T(8,128)(2,1)} %collective-permute-done.11.refs_6_.refs_2_.refs_0_, ...), custom_call_target="tpu_custom_call" | custom-call | flops 5452595200 | bytes 16056320 | tf_op jit(solution)/shard_map/pallas_call | solution.py:109
  256.4 16.0 %collective-permute-done.19 = f32[3,160,640]{2,1,0:T(8,128)} collective-permute-done((f32[3,160,640]{2,1,0:T(8,128)}, f32[3,160,640]{2,1,0:T(8,128)}, u32[]{:S(2)}, u32[]{:S(2)}) %collective-permute-start.19) | collective-permute-done | bytes 1228832 | tf_op jit(solution)/shard_map/ppermute | solution.py:32
  275.3 2.0 add.57
  278.9 11.7 %collective-permute-done.20 = bf16[3,160,640]{2,1,0:T(8,128)(2,1)} collective-permute-done((bf16[3,160,640]{2,1,0:T(8,128)(2,1)S(1)}, bf16[3,160,640]{2,1,0:T(8,128)(2,1)}, u32[]{:S(2)}, u32[]{:S(2)}) %collective-permute-start.20) | collective-permute-done | bytes 614432 | tf_op jit(solution)/shard_map/ppermute | solution.py:32
  292.0 2.0 add.63
  297.7 19.2 %collective-permute-done.14 = f32[3,160,640]{2,1,0:T(8,128)} collective-permute-done((f32[3,160,640]{2,1,0:T(8,128)}, f32[3,160,640]{2,1,0:T(8,128)}, u32[]{:S(2)}, u32[]{:S(2)}) %collective-permute-start.14) | collective-permute-done | bytes 1228832 | tf_op jit(solution)/shard_map/ppermute | solution.py:32
  320.2 12.8 %collective-permute-done.31 = f32[2,160,640]{2,1,0:T(8,128)S(1)} collective-permute-done((f32[2,160,640]{2,1,0:T(8,128)S(1)}, f32[2,160,640]{2,1,0:T(8,128)S(1)}, u32[]{:S(2)}, u32[]{:S(2)}) %collective-permute-start.31) | collective-permute-done | bytes 819232 | tf_op jit(solution)/shard_map/ppermute | solution.py:32
  335.2 13.4 %collective-permute-done.15 = bf16[1,160,640]{2,1,0:T(8,128)(2,1)S(1)} collective-permute-done((bf16[1,160,640]{2,1,0:T(8,128)(2,1)S(1)}, bf16[1,160,640]{2,1,0:T(8,128)(2,1)S(1)}, u32[]{:S(2)}, u32[]{:S(2)}) %collective-permute-start.15) | collective-permute-done | bytes 204832 | tf_op jit(solution)/shard_map/ppermute | solution.py:269
  348.5 2.6 collective-permute-start.17
  351.1 16.0 %shard_map.43.refs_4_ = f32[640,3328]{1,0:T(8,128)} custom-call(s32[1]{0:T(128)} %bitcast.high_ref._, bf16[3,320,640]{2,1,0:T(8,128)(2,1)} %copy-done.8, bf16[3,320,640]{2,1,0:T(8,128)(2,1)} %copy-done.10, bf16[640,1664]{1,0:T(8,128)(2,1)} %copy-done.6, bf16[640,1664]{1,0:T(8,128)(2,1)} %copy-done.5, ...), custom_call_target="tpu_custom_call" | custom-call | flops 8178892800 | bytes 23756800 | tf_op jit(solution)/shard_map/pallas_call | solution.py:181
  370.7 12.3 %collective-permute-done.22 = bf16[3,160,640]{2,1,0:T(8,128)(2,1)S(1)} collective-permute-done((bf16[3,160,640]{2,1,0:T(8,128)(2,1)S(1)}, bf16[3,160,640]{2,1,0:T(8,128)(2,1)S(1)}, u32[]{:S(2)}, u32[]{:S(2)}) %collective-permute-start.22) | collective-permute-done | bytes 614432 | tf_op jit(solution)/shard_map/ppermute | solution.py:32
  385.8 14.7 %shard_map.45.refs_4_ = f32[640,3328]{1,0:T(8,128)} custom-call(s32[1]{0:T(128)} %bitcast.high_ref._, bf16[2,320,640]{2,1,0:T(8,128)(2,1)} %copy-done.2, bf16[2,320,640]{2,1,0:T(8,128)(2,1)} %copy-done.9, bf16[640,1664]{1,0:T(8,128)(2,1)} %collective-permute-done.11.refs_6_.refs_2_.refs_0_, ...), custom_call_target="tpu_custom_call" | custom-call | flops 5452595200 | bytes 18677760 | tf_op jit(solution)/shard_map/pallas_call | solution.py:181
  400.5 16.2 %collective-permute-done.28.refs_0_ = bf16[640,1664]{1,0:T(8,128)(2,1)} collective-permute-done((bf16[640,1664]{1,0:T(8,128)(2,1)}, bf16[640,1664]{1,0:T(8,128)(2,1)}, u32[]{:S(2)}, u32[]{:S(2)}) %collective-permute-start.28) | collective-permute-done | bytes 2129952 | tf_op jit(solution)/shard_map/ppermute | solution.py:249
  419.3 18.7 %shard_map.46.refs_2_ = f32[640,3328]{1,0:T(8,128)} custom-call(s32[1]{0:T(128)} %bitcast.high_ref._, bf16[3,320,640]{2,1,0:T(8,128)(2,1)} %copy-done, bf16[3,320,640]{2,1,0:T(8,128)(2,1)} %copy-done.1, bf16[640,1664]{1,0:T(8,128)(2,1)} %collective-permute-done.28.refs_0_, bf16[640,1664]{1,0:T(8,128)(2,1)} %collective-permute-done.26.refs_1_, ...), custom_call_target="tpu_custom_call" | custom-call | flops 5452595200 | bytes 18677760 | tf_op jit(solution)/shard_map/pallas_call | solution.py:181
  438.1 23.0 %collective-permute-done.25.refs_0_ = bf16[640,1664]{1,0:T(8,128)(2,1)} collective-permute-done((bf16[640,1664]{1,0:T(8,128)(2,1)}, bf16[640,1664]{1,0:T(8,128)(2,1)}, u32[]{:S(2)}, u32[]{:S(2)}) %collective-permute-start.25) | collective-permute-done | bytes 2129952 | tf_op jit(solution)/shard_map/ppermute | solution.py:251
  461.1 11.8 %shard_map.47 = f32[640,3328]{1,0:T(8,128)} custom-call(s32[1]{0:T(128)} %bitcast.high_ref._, bf16[3,320,640]{2,1,0:T(8,128)(2,1)} %copy-done, bf16[3,320,640]{2,1,0:T(8,128)(2,1)} %copy-done.1, bf16[640,1664]{1,0:T(8,128)(2,1)} %collective-permute-done.25.refs_0_, bf16[640,1664]{1,0:T(8,128)(2,1)} %collective-permute-done.27.refs_1_, ...), custom_call_target="tpu_custom_call" | custom-call | flops 2726297600 | bytes 13598720 | tf_op jit(solution)/shard_map/pallas_call | solution.py:181
  (85 shorter events, 36.0 us)
Async XLA Ops:
  15.5 4.6 collective-permute-start.1
  25.1 3.8 collective-permute-start.3
  29.5 4.8 %collective-permute-start.4 = (f32[]{:T(128)}, f32[]{:T(128)}, u32[]{:S(2)}, u32[]{:S(2)}) collective-permute-start(f32[]{:T(128)} %add.54), channel_id=1, source_target_pairs={{0,16},{4,20},{8,24},{12,28},{16,0},{20,4},{24,8},{28,12},{1,17},{... | collective-permute-start | bytes 20 | tf_op jit(solution)/shard_map/ppermute | solution.py:32
  39.3 49.4 %collective-permute-start.9 = (bf16[640,1664]{1,0:T(8,128)(2,1)S(1)}, bf16[640,1664]{1,0:T(8,128)(2,1)}, u32[]{:S(2)}, u32[]{:S(2)}) collective-permute-start(bf16[640,1664]{1,0:T(8,128)(2,1)S(1)} %get-tuple-element.18.refs_1_), channel_id=1, source_target_pairs={{12,4},{20,12},{28,20},{24,28},{16,24},{8,16},{0,8},{4,0},{13,5},{... | collective-permute-start | bytes 6389768 | tf_op jit(solution)/shard_map/ppermute | solution.py:249
  41.3 49.3 %collective-permute-start.5 = (bf16[640,1664]{1,0:T(8,128)(2,1)S(1)}, bf16[640,1664]{1,0:T(8,128)(2,1)}, u32[]{:S(2)}, u32[]{:S(2)}) collective-permute-start(bf16[640,1664]{1,0:T(8,128)(2,1)S(1)} %get-tuple-element.19.refs_0_), channel_id=1, source_target_pairs={{4,12},{12,20},{20,28},{28,24},{24,16},{16,8},{8,0},{0,4},{5,13},{... | collective-permute-start | bytes 6389768 | tf_op jit(solution)/shard_map/ppermute | solution.py:249
  41.4 94.8 %collective-permute-start.6 = (bf16[640,1664]{1,0:T(8,128)(2,1)S(1)}, bf16[640,1664]{1,0:T(8,128)(2,1)}, u32[]{:S(2)}, u32[]{:S(2)}) collective-permute-start(bf16[640,1664]{1,0:T(8,128)(2,1)S(1)} %get-tuple-element.18.refs_1_), channel_id=1, source_target_pairs={{4,12},{12,20},{20,28},{28,24},{24,16},{16,8},{8,0},{0,4},{5,13},{... | collective-permute-start | bytes 6389768 | tf_op jit(solution)/shard_map/ppermute | solution.py:249
  43.2 93.1 %collective-permute-start.7 = (bf16[640,1664]{1,0:T(8,128)(2,1)S(1)}, bf16[640,1664]{1,0:T(8,128)(2,1)}, u32[]{:S(2)}, u32[]{:S(2)}) collective-permute-start(bf16[640,1664]{1,0:T(8,128)(2,1)S(1)} %get-tuple-element.19.refs_0_), channel_id=1, source_target_pairs={{12,4},{20,12},{28,20},{24,28},{16,24},{8,16},{0,8},{4,0},{13,5},{... | collective-permute-start | bytes 6389768 | tf_op jit(solution)/shard_map/ppermute | solution.py:249
  88.7 91.3 %collective-permute-start.10 = (bf16[640,1664]{1,0:T(8,128)(2,1)}, bf16[640,1664]{1,0:T(8,128)(2,1)}, u32[]{:S(2)}, u32[]{:S(2)}) collective-permute-start(bf16[640,1664]{1,0:T(8,128)(2,1)} %collective-permute-done.9.refs_5_), channel_id=1, source_target_pairs={{12,4},{20,12},{28,20},{24,28},{16,24},{8,16},{0,8},{4,0},{13,5},{... | collective-permute-start | bytes 6389768 | tf_op jit(solution)/shard_map/ppermute | solution.py:249
  90.6 91.3 %collective-permute-start.11 = (bf16[640,1664]{1,0:T(8,128)(2,1)}, bf16[640,1664]{1,0:T(8,128)(2,1)}, u32[]{:S(2)}, u32[]{:S(2)}) collective-permute-start(bf16[640,1664]{1,0:T(8,128)(2,1)} %collective-permute-done.5.refs_0_.refs_2_), channel_id=1, source_target_pairs={{4,12},{12,20},{20,28},{28,24},{24,16},{16,8},{8,0},{0,4},{5,13},{... | collective-permute-start | bytes 6389768 | tf_op jit(solution)/shard_map/ppermute | solution.py:249
  136.2 85.0 %collective-permute-start.12 = (bf16[640,1664]{1,0:T(8,128)(2,1)}, bf16[640,1664]{1,0:T(8,128)(2,1)}, u32[]{:S(2)}, u32[]{:S(2)}) collective-permute-start(bf16[640,1664]{1,0:T(8,128)(2,1)} %collective-permute-done.6.refs_1_.refs_3_), channel_id=1, source_target_pairs={{4,12},{12,20},{20,28},{28,24},{24,16},{16,8},{8,0},{0,4},{5,13},{... | collective-permute-start | bytes 6389768 | tf_op jit(solution)/shard_map/ppermute | solution.py:249
  136.4 84.9 %collective-permute-start.8 = (bf16[640,1664]{1,0:T(8,128)(2,1)}, bf16[640,1664]{1,0:T(8,128)(2,1)}, u32[]{:S(2)}, u32[]{:S(2)}) collective-permute-start(bf16[640,1664]{1,0:T(8,128)(2,1)} %collective-permute-done.7.refs_4_), channel_id=1, source_target_pairs={{12,4},{20,12},{28,20},{24,28},{16,24},{8,16},{0,8},{4,0},{13,5},{... | collective-permute-start | bytes 6389768 | tf_op jit(solution)/shard_map/ppermute | solution.py:249
  155.1 82.3 %collective-permute-start.18 = (f32[3,320,640]{2,1,0:T(8,128)}, f32[3,320,640]{2,1,0:T(8,128)S(1)}, u32[]{:S(2)}, u32[]{:S(2)}) collective-permute-start(f32[3,320,640]{2,1,0:T(8,128)} %get-tuple-element.12), channel_id=1, source_target_pairs={{0,1},{1,0},{2,3},{3,2},{4,5},{5,4},{6,7},{7,6},{8,9},{9,8},{10,11... | collective-permute-start | bytes 7372808 | tf_op jit(solution)/shard_map/ppermute | solution.py:32
  237.3 38.0 %collective-permute-start.13 = (f32[3,320,640]{2,1,0:T(8,128)}, f32[3,320,640]{2,1,0:T(8,128)}, u32[]{:S(2)}, u32[]{:S(2)}) collective-permute-start(f32[3,320,640]{2,1,0:T(8,128)} %get-tuple-element.10), channel_id=1, source_target_pairs={{0,1},{1,0},{2,3},{3,2},{4,5},{5,4},{6,7},{7,6},{8,9},{9,8},{10,11... | collective-permute-start | bytes 7372808 | tf_op jit(solution)/shard_map/ppermute | solution.py:32
  242.6 29.7 %collective-permute-start.19 = (f32[3,160,640]{2,1,0:T(8,128)}, f32[3,160,640]{2,1,0:T(8,128)}, u32[]{:S(2)}, u32[]{:S(2)}) collective-permute-start(f32[3,160,640]{2,1,0:T(8,128)} %constant_dynamic-slice_fusion.1), channel_id=1, source_target_pairs={{0,2},{1,3},{2,0},{3,1},{4,6},{5,7},{6,4},{7,5},{8,10},{9,11},{10,... | collective-permute-start | bytes 3686408 | tf_op jit(solution)/shard_map/ppermute | solution.py:32
  256.1 35.9 %collective-permute-start.30 = (f32[2,320,640]{2,1,0:T(8,128)}, f32[2,320,640]{2,1,0:T(8,128)}, u32[]{:S(2)}, u32[]{:S(2)}) collective-permute-start(f32[2,320,640]{2,1,0:T(8,128)} %get-tuple-element.15), channel_id=1, source_target_pairs={{0,1},{1,0},{2,3},{3,2},{4,5},{5,4},{6,7},{7,6},{8,9},{9,8},{10,11... | collective-permute-start | bytes 4915208 | tf_op jit(solution)/shard_map/ppermute | solution.py:32
  273.7 16.9 %collective-permute-start.20 = (bf16[3,160,640]{2,1,0:T(8,128)(2,1)S(1)}, bf16[3,160,640]{2,1,0:T(8,128)(2,1)}, u32[]{:S(2)}, u32[]{:S(2)}) collective-permute-start(bf16[3,160,640]{2,1,0:T(8,128)(2,1)S(1)} %add_convert_fusion), channel_id=1, source_target_pairs={{0,2},{1,3},{2,0},{3,1},{4,6},{5,7},{6,4},{7,5},{8,10},{9,11},{10,... | collective-permute-start | bytes 1843208 | tf_op jit(solution)/shard_map/ppermute | solution.py:32
  278.4 38.5 %collective-permute-start.14 = (f32[3,160,640]{2,1,0:T(8,128)}, f32[3,160,640]{2,1,0:T(8,128)}, u32[]{:S(2)}, u32[]{:S(2)}) collective-permute-start(f32[3,160,640]{2,1,0:T(8,128)} %constant_dynamic-slice_fusion.2), channel_id=1, source_target_pairs={{0,2},{1,3},{2,0},{3,1},{4,6},{5,7},{6,4},{7,5},{8,10},{9,11},{10,... | collective-permute-start | bytes 3686408 | tf_op jit(solution)/shard_map/ppermute | solution.py:32
  291.9 42.8 %collective-permute-start.21 = (bf16[3,320,640]{2,1,0:T(8,128)(2,1)S(1)}, bf16[3,320,640]{2,1,0:T(8,128)(2,1)S(1)}, u32[]{:S(2)}, u32[]{:S(2)}) collective-permute-start(bf16[3,320,640]{2,1,0:T(8,128)(2,1)S(1)} %pad_maximum_fusion.mine), channel_id=1, source_target_pairs={{0,1},{1,0},{2,3},{3,2},{4,5},{5,4},{6,7},{7,6},{8,9},{9,8},{10,11... | collective-permute-start | bytes 3686408 | tf_op jit(solution)/shard_map/ppermute | solution.py:32
  294.1 38.9 %collective-permute-start.31 = (f32[2,160,640]{2,1,0:T(8,128)S(1)}, f32[2,160,640]{2,1,0:T(8,128)S(1)}, u32[]{:S(2)}, u32[]{:S(2)}) collective-permute-start(f32[2,160,640]{2,1,0:T(8,128)S(1)} %constant_dynamic-slice_fusion), channel_id=1, source_target_pairs={{0,2},{1,3},{2,0},{3,1},{4,6},{5,7},{6,4},{7,5},{8,10},{9,11},{10,... | collective-permute-start | bytes 2457608 | tf_op jit(solution)/shard_map/ppermute | solution.py:32
  295.7 74.4 %collective-permute-start.24 = (bf16[640,1664]{1,0:T(8,128)(2,1)}, bf16[640,1664]{1,0:T(8,128)(2,1)}, u32[]{:S(2)}, u32[]{:S(2)}) collective-permute-start(bf16[640,1664]{1,0:T(8,128)(2,1)} %collective-permute-done.11.refs_6_.refs_2_.refs_0_), channel_id=1, source_target_pairs={{4,12},{12,20},{20,28},{28,24},{24,16},{16,8},{8,0},{0,4},{5,13},{... | collective-permute-start | bytes 6389768 | tf_op jit(solution)/shard_map/ppermute | solution.py:249
  296.1 74.0 %collective-permute-start.26 = (bf16[640,1664]{1,0:T(8,128)(2,1)}, bf16[640,1664]{1,0:T(8,128)(2,1)}, u32[]{:S(2)}, u32[]{:S(2)}) collective-permute-start(bf16[640,1664]{1,0:T(8,128)(2,1)} %collective-permute-done.10.refs_3_.refs_5_), channel_id=1, source_target_pairs={{12,4},{20,12},{28,20},{24,28},{16,24},{8,16},{0,8},{4,0},{13,5},{... | collective-permute-start | bytes 6389768 | tf_op jit(solution)/shard_map/ppermute | solution.py:249
  318.4 30.1 %collective-permute-start.15 = (bf16[1,160,640]{2,1,0:T(8,128)(2,1)S(1)}, bf16[1,160,640]{2,1,0:T(8,128)(2,1)S(1)}, u32[]{:S(2)}, u32[]{:S(2)}) collective-permute-start(bf16[1,160,640]{2,1,0:T(8,128)(2,1)S(1)} %get-tuple-element.26), channel_id=1, source_target_pairs={{4,0},{12,4},{20,12},{28,20},{24,28},{16,24},{8,16},{0,8},{5,1},{1... | collective-permute-start | bytes 614408 | tf_op jit(solution)/shard_map/ppermute | solution.py:269
  333.1 36.2 %collective-permute-start.32 = (bf16[2,160,640]{2,1,0:T(8,128)(2,1)S(1)}, bf16[2,160,640]{2,1,0:T(8,128)(2,1)S(1)}, u32[]{:S(2)}, u32[]{:S(2)}) collective-permute-start(bf16[2,160,640]{2,1,0:T(8,128)(2,1)S(1)} %add_convert_fusion.2), channel_id=1, source_target_pairs={{0,2},{1,3},{2,0},{3,1},{4,6},{5,7},{6,4},{7,5},{8,10},{9,11},{10,... | collective-permute-start | bytes 1228808 | tf_op jit(solution)/shard_map/ppermute | solution.py:32
  334.7 32.4 %collective-permute-start.16 = (bf16[1,160,640]{2,1,0:T(8,128)(2,1)S(1)}, bf16[1,160,640]{2,1,0:T(8,128)(2,1)S(1)}, u32[]{:S(2)}, u32[]{:S(2)}) collective-permute-start(bf16[1,160,640]{2,1,0:T(8,128)(2,1)S(1)} %get-tuple-element.28), channel_id=1, source_target_pairs={{4,12},{12,20},{20,28},{28,24},{24,16},{16,8},{8,0},{0,4},{5,13},{... | collective-permute-start | bytes 614408 | tf_op jit(solution)/shard_map/ppermute | solution.py:269
  348.5 20.2 %collective-permute-start.17 = (bf16[1,160,640]{2,1,0:T(8,128)(2,1)S(1)}, bf16[1,160,640]{2,1,0:T(8,128)(2,1)S(1)}, u32[]{:S(2)}, u32[]{:S(2)}) collective-permute-start(bf16[1,160,640]{2,1,0:T(8,128)(2,1)S(1)} %get-tuple-element.27), channel_id=1, source_target_pairs={{4,8},{12,0},{20,4},{28,12},{24,20},{16,28},{8,24},{0,16},{5,9},{1... | collective-permute-start | bytes 614408 | tf_op jit(solution)/shard_map/ppermute | solution.py:269
  367.1 49.6 %collective-permute-start.28 = (bf16[640,1664]{1,0:T(8,128)(2,1)}, bf16[640,1664]{1,0:T(8,128)(2,1)}, u32[]{:S(2)}, u32[]{:S(2)}) collective-permute-start(bf16[640,1664]{1,0:T(8,128)(2,1)} %collective-permute-done.8.refs_2_.refs_4_), channel_id=1, source_target_pairs={{12,4},{20,12},{28,20},{24,28},{16,24},{8,16},{0,8},{4,0},{13,5},{... | collective-permute-start | bytes 6389768 | tf_op jit(solution)/shard_map/ppermute | solution.py:249
  368.8 49.5 %collective-permute-start.29 = (bf16[640,1664]{1,0:T(8,128)(2,1)}, bf16[640,1664]{1,0:T(8,128)(2,1)}, u32[]{:S(2)}, u32[]{:S(2)}) collective-permute-start(bf16[640,1664]{1,0:T(8,128)(2,1)} %collective-permute-done.12.refs_7_.refs_3_.refs_1_), channel_id=1, source_target_pairs={{4,12},{12,20},{20,28},{28,24},{24,16},{16,8},{8,0},{0,4},{5,13},{... | collective-permute-start | bytes 6389768 | tf_op jit(solution)/shard_map/ppermute | solution.py:249
  369.3 13.7 %collective-permute-start.22 = (bf16[3,160,640]{2,1,0:T(8,128)(2,1)S(1)}, bf16[3,160,640]{2,1,0:T(8,128)(2,1)S(1)}, u32[]{:S(2)}, u32[]{:S(2)}) collective-permute-start(bf16[3,160,640]{2,1,0:T(8,128)(2,1)S(1)} %pad_maximum_fusion.3), channel_id=1, source_target_pairs={{0,2},{1,3},{2,0},{3,1},{4,6},{5,7},{6,4},{7,5},{8,10},{9,11},{10,... | collective-permute-start | bytes 1843208 | tf_op jit(solution)/shard_map/ppermute | solution.py:32
  370.1 14.8 %collective-permute-start.33 = (bf16[2,320,640]{2,1,0:T(8,128)(2,1)S(1)}, bf16[2,320,640]{2,1,0:T(8,128)(2,1)S(1)}, u32[]{:S(2)}, u32[]{:S(2)}) collective-permute-start(bf16[2,320,640]{2,1,0:T(8,128)(2,1)S(1)} %pad_maximum_fusion.2.mine), channel_id=1, source_target_pairs={{0,1},{1,0},{2,3},{3,2},{4,5},{5,4},{6,7},{7,6},{8,9},{9,8},{10,11... | collective-permute-start | bytes 2457608 | tf_op jit(solution)/shard_map/ppermute | solution.py:32
  370.1 91.0 %collective-permute-start.25 = (bf16[640,1664]{1,0:T(8,128)(2,1)}, bf16[640,1664]{1,0:T(8,128)(2,1)}, u32[]{:S(2)}, u32[]{:S(2)}) collective-permute-start(bf16[640,1664]{1,0:T(8,128)(2,1)} %collective-permute-done.24.refs_2_), channel_id=1, source_target_pairs={{4,12},{12,20},{20,28},{28,24},{24,16},{16,8},{8,0},{0,4},{5,13},{... | collective-permute-start | bytes 6389768 | tf_op jit(solution)/shard_map/ppermute | solution.py:251
  383.0 78.1 %collective-permute-start.27 = (bf16[640,1664]{1,0:T(8,128)(2,1)}, bf16[640,1664]{1,0:T(8,128)(2,1)}, u32[]{:S(2)}, u32[]{:S(2)}) collective-permute-start(bf16[640,1664]{1,0:T(8,128)(2,1)} %collective-permute-done.26.refs_1_), channel_id=1, source_target_pairs={{12,4},{20,12},{28,20},{24,28},{16,24},{8,16},{0,8},{4,0},{13,5},{... | collective-permute-start | bytes 6389768 | tf_op jit(solution)/shard_map/ppermute | solution.py:252
  384.9 33.4 %collective-permute-start.23 = (bf16[3,320,640]{2,1,0:T(8,128)(2,1)S(1)}, bf16[3,320,640]{2,1,0:T(8,128)(2,1)S(1)}, u32[]{:S(2)}, u32[]{:S(2)}) collective-permute-start(bf16[3,320,640]{2,1,0:T(8,128)(2,1)S(1)} %pad_maximum_fusion.1.mine), channel_id=1, source_target_pairs={{0,1},{1,0},{2,3},{3,2},{4,5},{5,4},{6,7},{7,6},{8,9},{9,8},{10,11... | collective-permute-start | bytes 3686408 | tf_op jit(solution)/shard_map/ppermute | solution.py:32
  (13 other events, 283.0 us)
